TPU v7x, 32 devices: a whole 2x2x4 slice. The times are simulated.
32 devices in a mesh: occ: 8 (over z, y), ao: 4 (over x, core).
Axes of the slice: x: 2, y: 2, z: 4, core: 2. Of those that a mesh axis runs over, the one named last changes fastest.
Arguments:
- amplitudes: bfloat16 [8, 640, 19456], P(None, 'occ', 'ao'), may hold values from -6 to 6
- occ_coef: bfloat16 [512, 640], P(None, 'occ'), may hold values from -0.25 to 0.25
- vir_coef: bfloat16 [512, 19456], P('occ', 'ao'), may hold values from -0.25 to 0.25
- occ_energy: float32 [640], P('occ'), may hold values from -1.5 to -0.3
- vir_energy: float32 [19456], P('ao'), may hold values from 0.05 to 2.5
- kernel: float32 [512], replicated, may hold values from 2 to 10
Outputs:
- residual: bfloat16 [8, 640, 19456], P(None, 'occ', 'ao')
- projected: float32 [8, 8], replicated
All inputs are finite; a program needn't handle non-finite values.
Results may differ from a plain program's by a relative error of at most 0.0049.
Values may be sent and summed in bfloat16 or wider, within the bound.
A program may use at most 128 MiB of HBM per device.

v0:
```python
import jax
import jax.numpy as jnp
from jax import lax
from jax.sharding import PartitionSpec as P


def shards(amplitudes, occ_coef, vir_coef, occ_energy, vir_energy, kernel):
    trials, occ_dev, vir_dev = amplitudes.shape
    row_total = occ_coef.shape[0]
    flat_amps = amplitudes.reshape(trials * occ_dev, vir_dev)
    occ_trans = occ_coef.T.astype(jnp.float32)
    whole_rows = lax.all_gather(vir_coef, "occ", axis=0, tiled=True)
    row_count = whole_rows.shape[0]
    half_done = lax.dot_general(
        flat_amps, whole_rows, (((1,), (1,)), ((), ())), preferred_element_type=jnp.float32
    )
    half_done = half_done.reshape(trials, occ_dev, row_count)
    partial_value = jnp.sum(half_done * occ_trans[None], axis=1)
    amps_rows = amplitudes.reshape(trials, occ_dev * vir_dev)
    density = lax.psum(partial_value, ("occ", "ao"))
    potential = kernel[None, :] * density
    weighted = (
        (occ_trans[None] * potential[:, None, :])
        .astype(jnp.bfloat16)
        .reshape(trials * occ_dev, row_total)
    )
    coupling = jnp.dot(weighted, whole_rows, preferred_element_type=jnp.float32)
    energy_gaps = vir_energy[None, :] - occ_energy[:, None]
    sigma_block = energy_gaps[None] * amplitudes.astype(jnp.float32) + coupling.reshape(
        trials, occ_dev, vir_dev
    )

    def gram_column(sigma_one):
        return jnp.sum(amplitudes.astype(jnp.float32) * sigma_one[None], axis=(1, 2))

    gram_local = lax.map(gram_column, sigma_block).T
    correlation_local = jnp.dot(amps_rows, amps_rows.T, preferred_element_type=jnp.float32)
    gram, correlation = lax.psum((gram_local, correlation_local), ("occ", "ao"))
    norms = jnp.diagonal(correlation) + 1e-06
    ritz_values = jnp.diagonal(gram) / norms
    residual = (sigma_block - ritz_values[:, None, None] * amplitudes.astype(jnp.float32)).astype(
        jnp.bfloat16
    )
    projected = gram / jnp.sqrt(norms[:, None] * norms[None, :])
    return (residual, projected)


def solution(mesh):
    placed = (P(None, "occ", "ao"), P(None, "occ"), P("occ", "ao"), P("occ"), P("ao"), P())
    return jax.shard_map(
        shards, mesh=mesh, in_specs=placed, out_specs=(P(None, "occ", "ao"), P()), check_vma=False
    )
```

profile of v0, /device:TPU:0, one launch (start us, length us, event | category | flops | bytes accessed | tf_op | source)
XLA Modules:
  0.0 258.6 jit_solution(4018655278099293986)
XLA Ops:
  7.2 0.0 copy-start.2
  7.2 0.0 copy-start
  7.2 0.0 all-gather.2.cloned.1.call-start
  7.2 0.7 all-gather.2.cloned.1.call-update
  7.9 0.9 convert_bitcast_fusion
  8.8 11.1 %fusion.14 = f32[8,8]{1,0:T(8,128)S(1)} fusion(bf16[8,80,4864]{2,1,0:T(8,128)(2,1)} %param.8), kind=kOutput, calls=%fused_computation.17 | convolution fusion | flops 49807360 | bytes 6226176 | tf_op jit(solution)/shard_map/dot_general | solution.py:37
  19.9 0.0 copy-done.2
  19.9 0.0 copy-done
  19.9 0.2 broadcast_subtract_fusion
  20.1 0.0 copy-start.1
  20.1 75.4 %all-gather.2.cloned.1.call-done = bf16[512,4864]{1,0:T(8,128)(2,1)} async-done(((bf16[64,4864]{1,0:T(8,128)(2,1)}), bf16[512,4864]{1,0:T(8,128)(2,1)}) %all-gather.2.cloned.1.call-update) | async-done | bytes 4980752 | tf_op jit(solution)/shard_map/all_gather | solution.py:12
  95.5 7.6 %fusion.11 = f32[8,512]{1,0:T(8,128)S(1)} fusion(bf16[8,80,4864]{2,1,0:T(8,128)(2,1)} %param.8, bf16[512,4864]{1,0:T(8,128)(2,1)} %all-gather.2.cloned.1.call-done, f32[80,512]{1,0:T(8,128)S(1)} %convert_bitcast_fusion), kind=kOutput, calls=%fused_computation.16 | convolution fusion | flops 3188322304 | bytes 11386880 | tf_op jit(solution)/shard_map/dot_general | solution.py:14
  103.2 38.8 %psum.21 = f32[8,512]{1,0:T(8,128)S(1)} all-reduce(f32[8,512]{1,0:T(8,128)S(1)} %fusion.11), channel_id=1, replica_groups=mesh['occ'=8,'ao'=4] {'occ','ao'}, use_global_device_ids=true, to_apply=%region_1.0 | all-reduce | flops 4096 | bytes 32768 | tf_op jit(solution)/shard_map/psum | solution.py:20
  141.9 0.0 copy-done.1
  142.0 9.7 %fusion = f32[8,80,4864]{2,1,0:T(8,128)} fusion(bf16[8,80,4864]{2,1,0:T(8,128)(2,1)} %param.8, f32[80,4864]{1,0:T(8,128)S(1)} %broadcast_subtract_fusion, bf16[512,4864]{1,0:T(8,128)(2,1)} %all-gather.2.cloned.1.call-done, f32[8,512]{1,0:T(8,128)S(1)} %broadcast_multiply_fusion, f32[80,512]{1,0:T(8,128)S(1)} %convert_bitcast_fusion), kind=kOutput, calls=%fused_computation.6 | convolution fusion | flops 3197665280 | bytes 25395200 | tf_op jit(solution)/shard_map/dot_general | solution.py:27
  151.7 46.7 %while.10 = (s32[]{:T(128)}, f32[8,8]{1,0:T(8,128)S(1)}, bf16[8,80,4864]{2,1,0:T(8,128)(2,1)}, f32[8,80,4864]{2,1,0:T(8,128)}, s32[]{:T(128)}, /*index=5*/s32[]{:T(128)}) while((s32[]{:T(128)}, f32[8,8]{1,0:T(8,128)S(1)}, bf16[8,80,4864]{2,1,0:T(8,128)(2,1)}, f32[8,80,4864]{2,1,0:T(8,128)}, s32[]{:T(128)}, /*index=5*/s32[]{:T(128)}) %tuple.23), condition=%wide.region_4.5_spmd, body=%wide.region_2.4_spmd.sunk | while | flops 9338874 | bytes 10895533 | solution.py:36
  151.7 1.5 dynamic-slice_bitcast_fusion.2
  153.2 4.3 %multiply_reduce_fusion.2 = f32[8]{0:T(128)S(1)} fusion(bf16[8,80,4864]{2,1,0:T(8,128)(2,1)} %get-tuple-element.76, f32[80,4864]{1,0:T(8,128)S(1)} %dynamic-slice_bitcast_fusion.2), kind=kLoop, calls=%fused_computation.2.clone.1 | loop fusion | flops 9338872 | bytes 7782432 | tf_op jit(solution)/shard_map/while/body/eval_jaxpr/reduce_sum | solution.py:34
  157.5 1.5 dynamic-slice_bitcast_fusion.2
  159.0 4.3 %multiply_reduce_fusion.2 = f32[8]{0:T(128)S(1)} fusion(bf16[8,80,4864]{2,1,0:T(8,128)(2,1)} %get-tuple-element.76, f32[80,4864]{1,0:T(8,128)S(1)} %dynamic-slice_bitcast_fusion.2), kind=kLoop, calls=%fused_computation.2.clone.1 | loop fusion | flops 9338872 | bytes 7782432 | tf_op jit(solution)/shard_map/while/body/eval_jaxpr/reduce_sum | solution.py:34
  163.3 1.5 dynamic-slice_bitcast_fusion.2
  164.8 4.3 %multiply_reduce_fusion.2 = f32[8]{0:T(128)S(1)} fusion(bf16[8,80,4864]{2,1,0:T(8,128)(2,1)} %get-tuple-element.76, f32[80,4864]{1,0:T(8,128)S(1)} %dynamic-slice_bitcast_fusion.2), kind=kLoop, calls=%fused_computation.2.clone.1 | loop fusion | flops 9338872 | bytes 7782432 | tf_op jit(solution)/shard_map/while/body/eval_jaxpr/reduce_sum | solution.py:34
  169.2 1.5 dynamic-slice_bitcast_fusion.2
  170.7 4.3 %multiply_reduce_fusion.2 = f32[8]{0:T(128)S(1)} fusion(bf16[8,80,4864]{2,1,0:T(8,128)(2,1)} %get-tuple-element.76, f32[80,4864]{1,0:T(8,128)S(1)} %dynamic-slice_bitcast_fusion.2), kind=kLoop, calls=%fused_computation.2.clone.1 | loop fusion | flops 9338872 | bytes 7782432 | tf_op jit(solution)/shard_map/while/body/eval_jaxpr/reduce_sum | solution.py:34
  175.0 1.5 dynamic-slice_bitcast_fusion.2
  176.5 4.3 %multiply_reduce_fusion.2 = f32[8]{0:T(128)S(1)} fusion(bf16[8,80,4864]{2,1,0:T(8,128)(2,1)} %get-tuple-element.76, f32[80,4864]{1,0:T(8,128)S(1)} %dynamic-slice_bitcast_fusion.2), kind=kLoop, calls=%fused_computation.2.clone.1 | loop fusion | flops 9338872 | bytes 7782432 | tf_op jit(solution)/shard_map/while/body/eval_jaxpr/reduce_sum | solution.py:34
  180.8 1.5 dynamic-slice_bitcast_fusion.2
  182.3 4.3 %multiply_reduce_fusion.2 = f32[8]{0:T(128)S(1)} fusion(bf16[8,80,4864]{2,1,0:T(8,128)(2,1)} %get-tuple-element.76, f32[80,4864]{1,0:T(8,128)S(1)} %dynamic-slice_bitcast_fusion.2), kind=kLoop, calls=%fused_computation.2.clone.1 | loop fusion | flops 9338872 | bytes 7782432 | tf_op jit(solution)/shard_map/while/body/eval_jaxpr/reduce_sum | solution.py:34
  186.7 1.5 dynamic-slice_bitcast_fusion.2
  188.2 4.3 %multiply_reduce_fusion.2 = f32[8]{0:T(128)S(1)} fusion(bf16[8,80,4864]{2,1,0:T(8,128)(2,1)} %get-tuple-element.76, f32[80,4864]{1,0:T(8,128)S(1)} %dynamic-slice_bitcast_fusion.2), kind=kLoop, calls=%fused_computation.2.clone.1 | loop fusion | flops 9338872 | bytes 7782432 | tf_op jit(solution)/shard_map/while/body/eval_jaxpr/reduce_sum | solution.py:34
  192.5 1.5 dynamic-slice_bitcast_fusion.2
  194.0 4.3 %multiply_reduce_fusion.2 = f32[8]{0:T(128)S(1)} fusion(bf16[8,80,4864]{2,1,0:T(8,128)(2,1)} %get-tuple-element.76, f32[80,4864]{1,0:T(8,128)S(1)} %dynamic-slice_bitcast_fusion.2), kind=kLoop, calls=%fused_computation.2.clone.1 | loop fusion | flops 9338872 | bytes 7782432 | tf_op jit(solution)/shard_map/while/body/eval_jaxpr/reduce_sum | solution.py:34
  198.3 0.1 copy.11
  198.4 40.7 %all-reduce = (f32[8,8]{1,0:T(8,128)S(1)}, f32[8,8]{1,0:T(8,128)S(1)}) all-reduce(f32[8,8]{1,0:T(8,128)S(1)} %bitcast.25, f32[8,8]{1,0:T(8,128)S(1)} %fusion.14), channel_id=1, replica_groups=mesh['occ'=8,'ao'=4] {'occ','ao'}, use_global_device_ids=true, to_apply=%region_5.6 | all-reduce | flops 128 | bytes 1024 | tf_op jit(solution)/shard_map/psum | solution.py:38
  239.1 0.6 gather_fusion
  239.7 0.6 gather_fusion.1
  240.4 0.7 rsqrt_multiply_fusion
  241.0 10.8 %fusion.2 = bf16[8,80,4864]{2,1,0:T(8,128)(2,1)} fusion(f32[8,80,4864]{2,1,0:T(8,128)} %get-tuple-element.82, bf16[8,80,4864]{2,1,0:T(8,128)(2,1)} %get-tuple-element.81, f32[8]{0:T(128)S(1)} %get-tuple-element.36), kind=kLoop, calls=%fused_computation.8 | loop fusion | flops 12451840 | bytes 24903712 | tf_op jit(solution)/shard_map/convert_element_type | solution.py:41
  (12 shorter events, 0.2 us)
Async XLA Ops:
  7.2 12.8 %copy-start.2 = (f32[80]{0:T(128)S(1)}, f32[80]{0:T(128)}, u32[]{:S(2)}) copy-start(f32[80]{0:T(128)} %param.11) | copy-start | bytes 964
  7.2 12.8 %copy-start = (f32[4864]{0:T(1024)S(1)}, f32[4864]{0:T(1024)}, u32[]{:S(2)}) copy-start(f32[4864]{0:T(1024)} %param.12) | copy-start | bytes 58372
  7.2 88.4 %all-gather.2.cloned.1.call-start = ((), (), s32[]{:S(2)}) async-start(), calls=%async_computation | async-start | bytes 5603328 | tf_op jit(solution)/shard_map/all_gather | solution.py:12
  20.1 121.8 %copy-start.1 = (f32[512]{0:T(512)S(1)}, f32[512]{0:T(512)}, u32[]{:S(2)}) copy-start(f32[512]{0:T(512)} %param.13) | copy-start | bytes 6148
Sparse Core Ops, SparseCore 0:
  10.2 85.3 all-gather.1
where the time goes:
time: 259 us
  blocking collectives  79.5 us (31%)
  waiting for transfers between devices  76.1 us (29%)
  other arithmetic  46.9 us (18%)
  matrix products  28.4 us (11%)
  between operations  14.1 us (5%)
  local copies, waits for them, and re-layouts  13.6 us (5%)
    all_gather x1, waiting for transfers between devices, shards(): whole_rows = lax.all_gather(vir_coef, 'occ', axis=0, tiled=True)  75.4 us
    psum x1, blocking collectives, shards(): gram, correlation = lax.psum((gram_local, correlation_local), ('occ', 'ao'))  40.7 us
    psum x1, blocking collectives, shards(): density = lax.psum(partial_value, ('occ', 'ao'))  38.8 us
    reduce_sum x8, other arithmetic, gram_column(): jnp.sum(amplitudes.astype(jnp.float32) * sigma_one[None], axis=(1, 2))  34.4 us
    mul x8, local copies, waits for them, and re-layouts, gram_column(): amplitudes.astype(jnp.float32) * sigma_one[None]  12.1 us
    dot_general x1, matrix products, shards(): jnp.dot(amps_rows, amps_rows.T, preferred_element_type=jnp.float32)  11.1 us
    convert_element_type x1, other arithmetic, shards(): (sigma_block - ritz_values[:, None, None] * amplitudes.astype(jnp.float32...  10.8 us
    dot_general x1, matrix products, shards(): coupling = jnp.dot(weighted, whole_rows, preferred_element_type=jnp.float32)  9.7 us
  transfers between devices with their start and end apart: 1, of which 1 were waited for; matrix products, arithmetic and copies ran while one was open for 5% of the time, Pallas kernels for 0%

commit v1 on v0

v1 whole, which is shorter than its diff:
```python
import functools

import jax
import jax.numpy as jnp
from jax import lax
from jax.experimental import pallas as pl
from jax.experimental.pallas import tpu as pltpu
from jax.sharding import PartitionSpec as P

LANES = 128
MESH = pl.DeviceIdType.MESH
F32 = jnp.float32


def split_tiles(first, last, parts):
    parts = min(parts, last - first)
    runs, at = [], first
    for j in range(parts):
        size = (last - at) // (parts - j)
        size += 1 if (last - at) % (parts - j) else 0
        runs.append((at * LANES, size * LANES))
        at += size
    return runs


def exchange(box, me, size, axis, send, recv):
    copies = []
    for d in range(1, size):
        copy = pltpu.make_async_remote_copy(
            src_ref=box.at[me],
            dst_ref=box.at[me],
            send_sem=send.at[d - 1],
            recv_sem=recv.at[me],
            device_id={axis: lax.rem(me + d, size)},
            device_id_type=MESH,
        )
        copy.start()
        copies.append(copy)
    for d in range(1, size):
        other = lax.rem(me + d, size)
        pltpu.make_async_remote_copy(
            src_ref=box.at[other],
            dst_ref=box.at[other],
            send_sem=send.at[d - 1],
            recv_sem=recv.at[other],
            device_id={axis: other},
            device_id_type=MESH,
        ).wait_recv()
    for copy in copies:
        copy.wait_send()


def gather_kernel(
    n,
    m,
    trials,
    runs,
    amps_hbm,
    vir_hbm,
    occ_ref,
    occ_energy_ref,
    vir_energy_ref,
    rows_hbm,
    stats_ref,
    amps,
    rows,
    dens,
    acc,
    box_ao,
    box_occ,
    local_sem,
    send_sem,
    recv_sem,
    ao_send,
    ao_recv,
    occ_send,
    occ_recv,
):
    own, col = lax.axis_index("occ"), lax.axis_index("ao")
    occ_dev = amps.shape[0] // trials
    tiles = amps.shape[1] // LANES
    total = n * rows.shape[1]
    pieces = len(runs[0])

    def place(p):
        back = p // (n // 2)
        return (1 - back) * 2 * p + back * (2 * (n - 1 - p) + 1)

    parity, half = lax.rem(own, 2), own // 2
    spot = parity * (n - 1 - half) + (1 - parity) * half
    toward = (place(lax.rem(spot + 1, n)), place(lax.rem(spot + n - 1, n)))

    take_rows = pltpu.make_async_copy(vir_hbm, rows.at[own], local_sem.at[0])
    take_rows.start()
    take_amps = pltpu.make_async_copy(amps_hbm, amps, local_sem.at[1])
    take_amps.start()

    barrier = pltpu.get_barrier_semaphore()
    for d in range(1, n):
        pl.semaphore_signal(
            barrier, inc=1, device_id={"occ": lax.rem(own + d, n)}, device_id_type=MESH
        )
    for d in range(1, m):
        pl.semaphore_signal(
            barrier, inc=1, device_id={"ao": lax.rem(col + d, m)}, device_id_type=MESH
        )
    pl.semaphore_wait(barrier, n + m - 2)
    take_rows.wait()

    def slot_of(way, age):
        if way == 0:
            return place(lax.rem(spot - age + n, n))
        return place(lax.rem(spot + age, n))

    def hop(way, j, slot, step):
        start, width = runs[way][j]
        piece = rows.at[slot, :, pl.ds(start, width)]
        return pltpu.make_async_remote_copy(
            src_ref=piece,
            dst_ref=piece,
            send_sem=send_sem.at[way, j, lax.rem(step, 2)],
            recv_sem=recv_sem.at[way, j, step],
            device_id={"occ": toward[way]},
            device_id_type=MESH,
        )

    def contract(way, j, slot):
        start, width = runs[way][j]
        half_done = lax.dot_general(
            amps[:, pl.ds(start, width)],
            rows[slot, :, pl.ds(start, width)],
            (((1,), (1,)), ((), ())),
            preferred_element_type=F32,
        )
        half_done = half_done.reshape(trials, occ_dev, rows.shape[1])
        dens[slot] += jnp.sum(half_done * occ_ref[slot][None], axis=1)

    pairs = [(k, l) for k in range(trials) for l in range(k, trials)]

    def fold(x):
        return jnp.sum(x.reshape(occ_dev // 8, 8, LANES), axis=0)

    def tally(tile):
        where = pl.ds(pl.multiple_of(tile * LANES, LANES), LANES)
        gap = vir_energy_ref[:, where] - occ_energy_ref[...]
        x = [amps[pl.ds(k * occ_dev, occ_dev), where].astype(F32) for k in range(trials)]
        at = 0
        for k in range(trials):
            scaled = gap * x[k]
            for l in range(k, trials):
                acc[2 * at] += fold(x[k] * x[l])
                acc[2 * at + 1] += fold(scaled * x[l])
                at += 1

    def finish_tally():
        row = lax.broadcasted_iota(jnp.int32, (trials, LANES), 0)
        lane = lax.broadcasted_iota(jnp.int32, (trials, LANES), 1)
        out = jnp.zeros((trials, LANES), F32)
        for at, (k, l) in enumerate(pairs):
            for part in range(2):
                value = jnp.sum(
                    jnp.sum(acc[2 * at + part], axis=0, keepdims=True), axis=1, keepdims=True
                )
                up = (row == k) & (lane == part * trials + l)
                down = (row == l) & (lane == part * trials + k)
                out = jnp.where(up | down, value, out)
        box_ao[col, :, pl.ds(total, LANES)] = out

    for way in range(2):
        for j in range(pieces):
            hop(way, j, own, 0).start()
    dens[...] = jnp.zeros_like(dens)
    acc[...] = jnp.zeros_like(acc)
    take_amps.wait()
    for way in range(2):
        for j in range(pieces):
            contract(way, j, own)

    slots = max((n - 2) * pieces, 1)
    per = -(-tiles // slots)

    def ring_step(step, carry):
        arrived = (slot_of(0, step + 1), slot_of(1, step + 1))
        for j in range(pieces):
            for way in range(2):
                hop(way, j, arrived[way], step).wait_recv()

                @pl.when(step < n - 2)
                def _():
                    @pl.when(step >= 1)
                    def _():
                        hop(way, j, arrived[way], step - 1).wait_send()

                    hop(way, j, arrived[way], step + 1).start()

            for way in range(2):
                contract(way, j, arrived[way])

            def unit(u, c):
                tile = (step * pieces + j) * per + u

                @pl.when(tile < tiles)
                def _():
                    tally(tile)

                return c

            lax.fori_loop(0, per, unit, 0)
            if j == 0:

                @pl.when(step == n - 2)
                def _():
                    finish_tally()

        return carry

    lax.fori_loop(0, n - 1, ring_step, 0)
    give_rows = pltpu.make_async_copy(rows, rows_hbm, local_sem.at[0])
    give_rows.start()
    box_ao[col, :, pl.ds(0, total)] = jnp.concatenate([dens[b] for b in range(n)], axis=1)
    exchange(box_ao, col, m, "ao", ao_send, ao_recv)
    value = box_ao[0]
    for d in range(1, m):
        value = value + box_ao[d]
    box_occ[own] = value
    exchange(box_occ, own, n, "occ", occ_send, occ_recv)
    value = box_occ[0]
    for d in range(1, n):
        value = value + box_occ[d]
    stats_ref[...] = value
    for way in range(2):
        for j in range(pieces):
            for step in range(max(n - 3, 0), n - 1):
                hop(way, j, own, step).wait_send()
    give_rows.wait()


def apply_kernel(
    trials,
    width,
    amps_hbm,
    rows_hbm,
    occ_ref,
    occ_energy_ref,
    vir_energy_ref,
    kernel_ref,
    stats_ref,
    out_hbm,
    projected_ref,
    amps,
    rows,
    out,
    weighted,
    shift,
    in_sem,
    out_sem,
):
    occ_dev = amps.shape[0] // trials
    total = rows.shape[0]
    count = amps.shape[1] // width

    def span(c):
        return pl.ds(pl.multiple_of(c * width, width), width)

    def take(c):
        return (
            pltpu.make_async_copy(rows_hbm.at[:, span(c)], rows.at[:, span(c)], in_sem.at[0, c]),
            pltpu.make_async_copy(amps_hbm.at[:, span(c)], amps.at[:, span(c)], in_sem.at[1, c]),
        )

    def give(c):
        return pltpu.make_async_copy(out.at[:, span(c)], out_hbm.at[:, span(c)], out_sem.at[c])

    for c in range(count):
        for copy in take(c):
            copy.start()

    density = stats_ref[:, pl.ds(0, total)]
    potential = kernel_ref[...] * density
    correlation = stats_ref[:, pl.ds(total, trials)]
    gram = stats_ref[:, pl.ds(total + trials, trials)]
    lane = lax.broadcasted_iota(jnp.int32, (trials, trials), 1)
    row = lax.broadcasted_iota(jnp.int32, (trials, trials), 0)
    for l in range(trials):
        coupled = jnp.sum(density * potential[l : l + 1], axis=1, keepdims=True)
        gram = gram + jnp.where(lane == l, coupled, 0.0)
    diagonal = jnp.where(lane == row, correlation + 1e-06, 0.0)
    norm_column = jnp.sum(diagonal, axis=1, keepdims=True)
    norm_row = jnp.sum(diagonal, axis=0, keepdims=True)
    projected_ref[...] = gram / jnp.sqrt(norm_column * norm_row)
    ritz = jnp.sum(jnp.where(lane == row, gram, 0.0), axis=1, keepdims=True) / norm_column
    for k in range(trials):
        own = pl.ds(k * occ_dev, occ_dev)
        weighted[own, :] = (occ_ref[...] * potential[k : k + 1]).astype(weighted.dtype)
        shift[own, :] = jnp.broadcast_to(
            occ_energy_ref[...] + ritz[k : k + 1], (occ_dev, LANES)
        )

    def block(c, carry):
        for copy in take(c):
            copy.wait()
        coupling = jnp.dot(weighted[...], rows[:, span(c)], preferred_element_type=F32)
        for t in range(width // LANES):
            here = pl.ds(pl.multiple_of(c * width + t * LANES, LANES), LANES)
            gap = vir_energy_ref[:, here] - shift[...]
            part = coupling[:, t * LANES : (t + 1) * LANES]
            out[:, here] = (gap * amps[:, here].astype(F32) + part).astype(out.dtype)
        give(c).start()
        return carry

    lax.fori_loop(0, count, block, 0)
    for c in range(count):
        give(c).wait()


def shards(n, m, amplitudes, occ_coef, vir_coef, occ_energy, vir_energy, kernel):
    trials, occ_dev, vir_dev = amplitudes.shape
    row_dev = vir_coef.shape[0]
    total = occ_coef.shape[0]
    flat = amplitudes.reshape(trials * occ_dev, vir_dev)
    tiles = vir_dev // LANES
    parts = 4 if n <= 16 else 1
    runs = (split_tiles(0, tiles // 2, parts), split_tiles(tiles // 2, tiles, parts))
    pieces = len(runs[0])
    length = total + LANES
    occ_trans = occ_coef.T.astype(F32)
    occ_blocks = jnp.transpose(occ_coef.reshape(n, row_dev, occ_dev), (0, 2, 1)).astype(F32)
    energy_column = occ_energy[:, None]
    energy_row = vir_energy[None, :]
    vmem = pl.BlockSpec(memory_space=pltpu.VMEM)
    any_space = pl.BlockSpec(memory_space=pl.ANY)
    dma = pltpu.SemaphoreType.DMA
    matmul_flops = 2 * trials * occ_dev * vir_dev * total
    rows, stats = pl.pallas_call(
        functools.partial(gather_kernel, n, m, trials, runs),
        out_shape=(
            jax.ShapeDtypeStruct((n, row_dev, vir_dev), vir_coef.dtype),
            jax.ShapeDtypeStruct((trials, length), F32),
        ),
        in_specs=[any_space, any_space, vmem, vmem, vmem],
        out_specs=(any_space, vmem),
        scratch_shapes=[
            pltpu.VMEM((trials * occ_dev, vir_dev), amplitudes.dtype),
            pltpu.VMEM((n, row_dev, vir_dev), vir_coef.dtype),
            pltpu.VMEM((n, trials, row_dev), F32),
            pltpu.VMEM((trials * (trials + 1), 8, LANES), F32),
            pltpu.VMEM((m, trials, length), F32),
            pltpu.VMEM((n, trials, length), F32),
            dma((2,)),
            dma((2, pieces, 2)),
            dma((2, pieces, n - 1)),
            dma((m - 1,)),
            dma((m,)),
            dma((n - 1,)),
            dma((n,)),
        ],
        compiler_params=pltpu.CompilerParams(collective_id=0, has_side_effects=True),
        cost_estimate=pl.CostEstimate(
            flops=matmul_flops, bytes_accessed=flat.size * 4, transcendentals=0
        ),
    )(flat, vir_coef, occ_blocks, energy_column, energy_row)
    width = 2 * LANES if tiles % 2 == 0 else LANES
    count = vir_dev // width
    residual, projected = pl.pallas_call(
        functools.partial(apply_kernel, trials, width),
        out_shape=(
            jax.ShapeDtypeStruct(flat.shape, amplitudes.dtype),
            jax.ShapeDtypeStruct((trials, trials), F32),
        ),
        in_specs=[any_space, any_space, vmem, vmem, vmem, vmem, vmem],
        out_specs=(any_space, vmem),
        scratch_shapes=[
            pltpu.VMEM(flat.shape, amplitudes.dtype),
            pltpu.VMEM((total, vir_dev), vir_coef.dtype),
            pltpu.VMEM(flat.shape, amplitudes.dtype),
            pltpu.VMEM((trials * occ_dev, total), jnp.bfloat16),
            pltpu.VMEM((trials * occ_dev, LANES), F32),
            dma((2, count)),
            dma((count,)),
        ],
        cost_estimate=pl.CostEstimate(
            flops=matmul_flops, bytes_accessed=flat.size * 6, transcendentals=0
        ),
    )(
        flat,
        rows.reshape(total, vir_dev),
        occ_trans,
        energy_column,
        energy_row,
        kernel[None, :],
        stats,
    )
    return residual.reshape(amplitudes.shape), projected


def solution(mesh):
    placed = (P(None, "occ", "ao"), P(None, "occ"), P("occ", "ao"), P("occ"), P("ao"), P())
    return jax.shard_map(
        functools.partial(shards, mesh.shape["occ"], mesh.shape["ao"]),
        mesh=mesh,
        in_specs=placed,
        out_specs=(P(None, "occ", "ao"), P()),
        check_vma=False,
    )
```

time: 259 us -> 82.5 us (0.32)
  blocking collectives: 79.5 us -> 0 us
  waiting for transfers between devices: 76.1 us -> 0 us
  Pallas kernels: 0 us -> 75.4 us
  other arithmetic: 46.9 us -> 1.57 us
  matrix products: 28.4 us -> 0 us
  between operations: 14.1 us -> 0.65 us
  local copies, waits for them, and re-layouts: 13.6 us -> 4.51 us
    psum x2 -> x0, blocking collectives: 79.5 us -> none  [the longest x1 40.7 us: shards(): gram, correlation = lax.psum((gram_local, correlation_local), ('occ', 'ao'))]
    pallas_call x0 -> x2, Pallas kernels: none -> 75.4 us  [the longest x1 64.8 us: shards(): pl.pallas_call(functools.partial(gather_kernel, n, m, trials, runs), out_...]
    all_gather x1 -> x0, waiting for transfers between devices: 75.4 us -> none  [shards(): whole_rows = lax.all_gather(vir_coef, 'occ', axis=0, tiled=True)]
    reduce_sum x8 -> x0, other arithmetic: 34.4 us -> none  [gram_column(): jnp.sum(amplitudes.astype(jnp.float32) * sigma_one[None], axis=(1, 2))]
    dot_general x3 -> x0, matrix products: 28.4 us -> none  [the longest x1 11.1 us: shards(): jnp.dot(amps_rows, amps_rows.T, preferred_element_type=jnp.float32)]
    mul x8 -> x0, local copies, waits for them, and re-layouts: 12.1 us -> none  [gram_column(): amplitudes.astype(jnp.float32) * sigma_one[None]]
    convert_element_type x2 -> x1, other arithmetic: 11.7 us -> 1.57 us  [shards(): occ_trans = occ_coef.T.astype(F32)]
    broadcast_in_dim x0 -> x2, local copies, waits for them, and re-layouts: none -> 2.71 us  [the longest x1 1.36 us: shards(): energy_column = occ_energy[:, None]]
  transfers between devices with their start and end apart: 1 -> 0, of which waited for: 1 -> 0; matrix products, arithmetic and copies ran while one was open for 5% -> 0% of each run, Pallas kernels for 0% -> 0%
where the time goes in v1:
time: 82.5 us; the launch traced here: 82.2 us
  Pallas kernels  75.4 us (91%)
  local copies, waits for them, and re-layouts  4.51 us (5%)
  other arithmetic  1.57 us (2%)
    pallas_call x1, Pallas kernels, shards(): pl.pallas_call(functools.partial(gather_kernel, n, m, trials, runs), out_...  64.8 us
    pallas_call x1, Pallas kernels, shards(): pl.pallas_call(functools.partial(apply_kernel, trials, width), out_shape=...  10.6 us
    convert_element_type x2, local copies, waits for them, and re-layouts, shards(): jnp.transpose(occ_coef.reshape(n, row_dev, occ_dev), (0, 2, 1)).astype(F32)  1.8 us

profile of v1, /device:TPU:0, one launch (start us, length us, event | category | flops | bytes accessed | tf_op | source)
XLA Modules:
  0.0 82.2 jit_solution(289031099068307321)
XLA Ops:
  0.6 1.4 %broadcast_in_dim.10.vir_energy_ref = f32[1,4864]{1,0:T(1,128)} reshape(f32[4864]{0:T(1024)} %param.10) | data formatting | bytes 38912 | tf_op jit(solution)/shard_map/broadcast_in_dim | solution.py:329
  2.0 1.4 %copy.12.occ_energy_ref = f32[80,1]{1,0:T(8,128)} copy(f32[80,1]{0,1:T(1,128)} %bitcast.13) | data formatting | bytes 640 | tf_op jit(solution)/shard_map/broadcast_in_dim | solution.py:328
  3.3 1.6 %convert_bitcast_fusion.occ_ref = f32[80,512]{1,0:T(8,128)} fusion(bf16[512,80]{0,1:T(8,128)(2,1)} %param.7), kind=kLoop, calls=%fused_computation.1 | loop fusion | flops 40960 | bytes 245760 | tf_op jit(solution)/shard_map/convert_element_type | solution.py:326
  4.9 1.0 %reshape.19 = f32[8,64,80]{1,0,2:T(8,128)S(1)} reshape(bf16[512,80]{0,1:T(8,128)(2,1)} %param.7) | data formatting | bytes 245760 | tf_op jit(solution)/shard_map/convert_element_type | solution.py:327
  5.9 0.8 copy.15
  6.7 64.8 %shard_map.77 = (bf16[8,64,4864]{2,1,0:T(8,128)(2,1)}, f32[8,640]{1,0:T(8,128)}) custom-call(bf16[640,4864]{1,0:T(8,128)(2,1)} %bitcast.14, bf16[64,4864]{1,0:T(8,128)(2,1)} %vir_hbm.1, f32[8,80,64]{2,1,0:T(8,128)} %bitcast.12, f32[80,1]{1,0:T(8,128)} %copy.12.occ_energy_ref, f32[1,4864]{1,0:T(1,128)} %broadcast_in_dim.10.vir_energy_ref), custom_call_target="tpu_custom_call" | custom-call | flops 3187671040 | bytes 12451840 | tf_op jit(solution)/shard_map/pallas_call | solution.py:334
  71.5 10.6 %shard_map.78 = (bf16[640,4864]{1,0:T(8,128)(2,1)}, f32[8,8]{1,0:T(8,128)}) custom-call(bf16[640,4864]{1,0:T(8,128)(2,1)} %bitcast.15, bf16[512,4864]{1,0:T(8,128)(2,1)} %bitcast.18, f32[80,512]{1,0:T(8,128)} %convert_bitcast_fusion.occ_ref, f32[80,1]{1,0:T(8,128)} %copy.12.occ_energy_ref, f32[1,4864]{1,0:T(1,128)} %broadcast_in_dim.10.vir_energy_ref, ...), custom_call_target="tpu_custom_call" | custom-call | flops 3187671040 | bytes 18677760 | tf_op jit(solution)/shard_map/pallas_call | solution.py:364

commit v2 on v1

--- a/solution.py
+++ b/solution.py
@@ -21,6 +21,13 @@
         runs.append((at * LANES, size * LANES))
         at += size
     return runs
+
+
+def as_column(row):
+    count = row.shape[1]
+    here = lax.broadcasted_iota(jnp.int32, (count, count), 0)
+    lane = lax.broadcasted_iota(jnp.int32, (count, count), 1)
+    return jnp.sum(jnp.where(here == lane, row, 0.0), axis=1, keepdims=True)
 
 
 def exchange(box, me, size, axis, send, recv):
@@ -66,6 +73,8 @@
     rows,
     dens,
     acc,
+    occ_blocks,
+    energy_column,
     box_ao,
     box_occ,
     local_sem,
@@ -93,7 +102,6 @@
     take_rows = pltpu.make_async_copy(vir_hbm, rows.at[own], local_sem.at[0])
     take_rows.start()
     take_amps = pltpu.make_async_copy(amps_hbm, amps, local_sem.at[1])
-    take_amps.start()
 
     barrier = pltpu.get_barrier_semaphore()
     for d in range(1, n):
@@ -104,8 +112,9 @@
         pl.semaphore_signal(
             barrier, inc=1, device_id={"ao": lax.rem(col + d, m)}, device_id_type=MESH
         )
+    take_rows.wait()
+    take_amps.start()
     pl.semaphore_wait(barrier, n + m - 2)
-    take_rows.wait()
 
     def slot_of(way, age):
         if way == 0:
@@ -133,7 +142,7 @@
             preferred_element_type=F32,
         )
         half_done = half_done.reshape(trials, occ_dev, rows.shape[1])
-        dens[slot] += jnp.sum(half_done * occ_ref[slot][None], axis=1)
+        dens[slot] += jnp.sum(half_done * occ_blocks[slot][None], axis=1)
 
     pairs = [(k, l) for k in range(trials) for l in range(k, trials)]
 
@@ -142,7 +151,7 @@
 
     def tally(tile):
         where = pl.ds(pl.multiple_of(tile * LANES, LANES), LANES)
-        gap = vir_energy_ref[:, where] - occ_energy_ref[...]
+        gap = vir_energy_ref[where][None, :] - energy_column[...]
         x = [amps[pl.ds(k * occ_dev, occ_dev), where].astype(F32) for k in range(trials)]
         at = 0
         for k in range(trials):
@@ -171,6 +180,11 @@
             hop(way, j, own, 0).start()
     dens[...] = jnp.zeros_like(dens)
     acc[...] = jnp.zeros_like(acc)
+    occ_float = occ_ref[...].astype(F32)
+    row_dev = rows.shape[1]
+    for b in range(n):
+        occ_blocks[b] = occ_float[:, b * row_dev : (b + 1) * row_dev]
+    energy_column[...] = jnp.broadcast_to(as_column(occ_energy_ref[...]), (occ_dev, LANES))
     take_amps.wait()
     for way in range(2):
         for j in range(pieces):
@@ -271,7 +285,8 @@
     def give(c):
         return pltpu.make_async_copy(out.at[:, span(c)], out_hbm.at[:, span(c)], out_sem.at[c])
 
-    for c in range(count):
+    ahead = min(6, count)
+    for c in range(ahead):
         for copy in take(c):
             copy.start()
 
@@ -289,26 +304,48 @@
     norm_row = jnp.sum(diagonal, axis=0, keepdims=True)
     projected_ref[...] = gram / jnp.sqrt(norm_column * norm_row)
     ritz = jnp.sum(jnp.where(lane == row, gram, 0.0), axis=1, keepdims=True) / norm_column
+    occ_float = occ_ref[...].astype(F32)
+    energy_column = as_column(occ_energy_ref[...])
     for k in range(trials):
         own = pl.ds(k * occ_dev, occ_dev)
-        weighted[own, :] = (occ_ref[...] * potential[k : k + 1]).astype(weighted.dtype)
-        shift[own, :] = jnp.broadcast_to(
-            occ_energy_ref[...] + ritz[k : k + 1], (occ_dev, LANES)
-        )
-
-    def block(c, carry):
-        for copy in take(c):
-            copy.wait()
-        coupling = jnp.dot(weighted[...], rows[:, span(c)], preferred_element_type=F32)
-        for t in range(width // LANES):
-            here = pl.ds(pl.multiple_of(c * width + t * LANES, LANES), LANES)
-            gap = vir_energy_ref[:, here] - shift[...]
-            part = coupling[:, t * LANES : (t + 1) * LANES]
-            out[:, here] = (gap * amps[:, here].astype(F32) + part).astype(out.dtype)
-        give(c).start()
+        weighted[own, :] = (occ_float * potential[k : k + 1]).astype(weighted.dtype)
+        shift[own, :] = jnp.broadcast_to(energy_column + ritz[k : k + 1], (occ_dev, LANES))
+
+    def blocks(first, size):
+        for c in range(size):
+            later = first + c + ahead
+
+            @pl.when(later < count)
+            def _():
+                for copy in take(later):
+                    copy.start()
+
+        for c in range(size):
+            for copy in take(first + c):
+                copy.wait()
+        for c in range(size):
+            at = (first + c) * width
+            coupling = jnp.dot(
+                weighted[...], rows[:, span(first + c)], preferred_element_type=F32
+            )
+            for t in range(width // LANES):
+                here = pl.ds(pl.multiple_of(at + t * LANES, LANES), LANES)
+                gap = vir_energy_ref[here][None, :] - shift[...]
+                part = coupling[:, t * LANES : (t + 1) * LANES]
+                out[:, here] = (gap * amps[:, here].astype(F32) + part).astype(out.dtype)
+        for c in range(size):
+            give(first + c).start()
+
+    group = 3
+    lead = count % group
+    if lead:
+        blocks(0, lead)
+
+    def turn(g, carry):
+        blocks(lead + g * group, group)
         return carry
 
-    lax.fori_loop(0, count, block, 0)
+    lax.fori_loop(0, count // group, turn, 0)
     for c in range(count):
         give(c).wait()
 
@@ -323,10 +360,8 @@
     runs = (split_tiles(0, tiles // 2, parts), split_tiles(tiles // 2, tiles, parts))
     pieces = len(runs[0])
     length = total + LANES
-    occ_trans = occ_coef.T.astype(F32)
-    occ_blocks = jnp.transpose(occ_coef.reshape(n, row_dev, occ_dev), (0, 2, 1)).astype(F32)
-    energy_column = occ_energy[:, None]
-    energy_row = vir_energy[None, :]
+    occ_trans = occ_coef.T
+    energy_row = occ_energy[None, :]
     vmem = pl.BlockSpec(memory_space=pltpu.VMEM)
     any_space = pl.BlockSpec(memory_space=pl.ANY)
     dma = pltpu.SemaphoreType.DMA
@@ -344,6 +379,8 @@
             pltpu.VMEM((n, row_dev, vir_dev), vir_coef.dtype),
             pltpu.VMEM((n, trials, row_dev), F32),
             pltpu.VMEM((trials * (trials + 1), 8, LANES), F32),
+            pltpu.VMEM((n, occ_dev, row_dev), F32),
+            pltpu.VMEM((occ_dev, LANES), F32),
             pltpu.VMEM((m, trials, length), F32),
             pltpu.VMEM((n, trials, length), F32),
             dma((2,)),
@@ -358,7 +395,7 @@
         cost_estimate=pl.CostEstimate(
             flops=matmul_flops, bytes_accessed=flat.size * 4, transcendentals=0
         ),
-    )(flat, vir_coef, occ_blocks, energy_column, energy_row)
+    )(flat, vir_coef, occ_trans, energy_row, vir_energy)
     width = 2 * LANES if tiles % 2 == 0 else LANES
     count = vir_dev // width
     residual, projected = pl.pallas_call(
@@ -385,8 +422,8 @@
         flat,
         rows.reshape(total, vir_dev),
         occ_trans,
-        energy_column,
         energy_row,
+        vir_energy,
         kernel[None, :],
         stats,
     )

time: 82.5 us -> 75.8 us (0.919)
  local copies, waits for them, and re-layouts: 4.51 us -> 0 us
  other arithmetic: 1.57 us -> 0 us
    broadcast_in_dim x2 -> x0, local copies, waits for them, and re-layouts: 2.71 us -> none  [the longest x1 1.36 us: shards(): energy_column = occ_energy[:, None]]
    convert_element_type x2 -> x0, local copies, waits for them, and re-layouts: 1.8 us -> none  [shards(): jnp.transpose(occ_coef.reshape(n, row_dev, occ_dev), (0, 2, 1)).astype(F32)]
    convert_element_type x1 -> x0, other arithmetic: 1.57 us -> none  [shards(): occ_trans = occ_coef.T.astype(F32)]
where the time goes in v2:
time: 75.8 us; the launch traced here: 75.5 us
  Pallas kernels  74.9 us (99%)
    pallas_call x1, Pallas kernels, shards(): pl.pallas_call(functools.partial(gather_kernel, n, m, trials, runs), out_...  64.7 us
    pallas_call x1, Pallas kernels, shards(): pl.pallas_call(functools.partial(apply_kernel, trials, width), out_shape=...  10.2 us

profile of v2, /device:TPU:0, one launch (start us, length us, event | category | flops | bytes accessed | tf_op | source)
XLA Modules:
  0.0 75.5 jit_solution(554944568115869515)
XLA Ops:
  0.6 64.7 %shard_map.77 = (bf16[8,64,4864]{2,1,0:T(8,128)(2,1)}, f32[8,640]{1,0:T(8,128)}) custom-call(bf16[640,4864]{1,0:T(8,128)(2,1)} %bitcast.6, bf16[64,4864]{1,0:T(8,128)(2,1)} %vir_hbm.1, bf16[80,512]{1,0:T(8,128)(2,1)} %bitcast.8, f32[1,80]{1,0:T(1,128)} %bitcast.11, f32[4864]{0:T(1024)} %vir_energy_ref.3), custom_call_target="tpu_custom_call" | custom-call | flops 3187671040 | bytes 12451840 | tf_op jit(solution)/shard_map/pallas_call | solution.py:369
  65.3 10.2 %shard_map.78 = (bf16[640,4864]{1,0:T(8,128)(2,1)}, f32[8,8]{1,0:T(8,128)}) custom-call(bf16[640,4864]{1,0:T(8,128)(2,1)} %bitcast.7, bf16[512,4864]{1,0:T(8,128)(2,1)} %bitcast.14, bf16[80,512]{1,0:T(8,128)(2,1)} %bitcast.9, f32[1,80]{1,0:T(1,128)} %bitcast.12, f32[4864]{0:T(1024)} %vir_energy_ref.3, f32[1,512]{1,0:T(1,128)} %bitcast.10, ...), custom_call_target="tpu_custom_call" | custom-call | flops 3187671040 | bytes 18677760 | tf_op jit(solution)/shard_map/pallas_call | solution.py:401

commit v3 on v2

--- a/solution.py
+++ b/solution.py
@@ -273,21 +273,33 @@
     total = rows.shape[0]
     count = amps.shape[1] // width
 
-    def span(c):
-        return pl.ds(pl.multiple_of(c * width, width), width)
-
-    def take(c):
+    group = 3
+    lead = count % group
+    turns = count // group
+
+    def span(c, size=1):
+        return pl.ds(pl.multiple_of(c * width, width), size * width)
+
+    def take(first, size, sem):
+        here = span(first, size)
         return (
-            pltpu.make_async_copy(rows_hbm.at[:, span(c)], rows.at[:, span(c)], in_sem.at[0, c]),
-            pltpu.make_async_copy(amps_hbm.at[:, span(c)], amps.at[:, span(c)], in_sem.at[1, c]),
-        )
-
-    def give(c):
-        return pltpu.make_async_copy(out.at[:, span(c)], out_hbm.at[:, span(c)], out_sem.at[c])
-
-    ahead = min(6, count)
-    for c in range(ahead):
-        for copy in take(c):
+            pltpu.make_async_copy(rows_hbm.at[:, here], rows.at[:, here], in_sem.at[0, sem]),
+            pltpu.make_async_copy(amps_hbm.at[:, here], amps.at[:, here], in_sem.at[1, sem]),
+        )
+
+    def give(first, size, sem):
+        here = span(first, size)
+        return pltpu.make_async_copy(out.at[:, here], out_hbm.at[:, here], out_sem.at[sem])
+
+    def take_turn(g):
+        return take(lead + g * group, group, g)
+
+    ahead = min(3, turns)
+    if lead:
+        for copy in take(0, lead, turns):
+            copy.start()
+    for g in range(ahead):
+        for copy in take_turn(g):
             copy.start()
 
     density = stats_ref[:, pl.ds(0, total)]
@@ -313,17 +325,6 @@
 
     def blocks(first, size):
         for c in range(size):
-            later = first + c + ahead
-
-            @pl.when(later < count)
-            def _():
-                for copy in take(later):
-                    copy.start()
-
-        for c in range(size):
-            for copy in take(first + c):
-                copy.wait()
-        for c in range(size):
             at = (first + c) * width
             coupling = jnp.dot(
                 weighted[...], rows[:, span(first + c)], preferred_element_type=F32
@@ -333,21 +334,30 @@
                 gap = vir_energy_ref[here][None, :] - shift[...]
                 part = coupling[:, t * LANES : (t + 1) * LANES]
                 out[:, here] = (gap * amps[:, here].astype(F32) + part).astype(out.dtype)
-        for c in range(size):
-            give(first + c).start()
-
-    group = 3
-    lead = count % group
+
     if lead:
+        for copy in take(0, lead, turns):
+            copy.wait()
         blocks(0, lead)
+        give(0, lead, turns).start()
 
     def turn(g, carry):
+        @pl.when(g + ahead < turns)
+        def _():
+            for copy in take_turn(g + ahead):
+                copy.start()
+
+        for copy in take_turn(g):
+            copy.wait()
         blocks(lead + g * group, group)
+        give(lead + g * group, group, g).start()
         return carry
 
-    lax.fori_loop(0, count // group, turn, 0)
-    for c in range(count):
-        give(c).wait()
+    lax.fori_loop(0, turns, turn, 0)
+    if lead:
+        give(0, lead, turns).wait()
+    for g in range(turns):
+        give(lead + g * group, group, g).wait()
 
 
 def shards(n, m, amplitudes, occ_coef, vir_coef, occ_energy, vir_energy, kernel):
@@ -412,8 +422,8 @@
             pltpu.VMEM(flat.shape, amplitudes.dtype),
             pltpu.VMEM((trials * occ_dev, total), jnp.bfloat16),
             pltpu.VMEM((trials * occ_dev, LANES), F32),
-            dma((2, count)),
-            dma((count,)),
+            dma((2, count // 3 + 1)),
+            dma((count // 3 + 1,)),
         ],
         cost_estimate=pl.CostEstimate(
             flops=matmul_flops, bytes_accessed=flat.size * 6, transcendentals=0

time: 75.8 us -> 74.7 us (0.985)
  Pallas kernels: 74.9 us -> 73.7 us
    pallas_call x1, Pallas kernels: 10.2 us -> 9.06 us  [shards(): pl.pallas_call(functools.partial(apply_kernel, trials, width), out_shape=...]
where the time goes in v3:
time: 74.7 us; the launch traced here: 74.4 us
  Pallas kernels  73.7 us (99%)
    pallas_call x1, Pallas kernels, shards(): pl.pallas_call(functools.partial(gather_kernel, n, m, trials, runs), out_...  64.7 us
    pallas_call x1, Pallas kernels, shards(): pl.pallas_call(functools.partial(apply_kernel, trials, width), out_shape=...  9.06 us

profile of v3, /device:TPU:0, one launch (start us, length us, event | category | flops | bytes accessed | tf_op | source)
XLA Modules:
  0.0 74.4 jit_solution(9394768398966805501)
XLA Ops:
  0.6 64.7 %shard_map.77 = (bf16[8,64,4864]{2,1,0:T(8,128)(2,1)}, f32[8,640]{1,0:T(8,128)}) custom-call(bf16[640,4864]{1,0:T(8,128)(2,1)} %bitcast.6, bf16[64,4864]{1,0:T(8,128)(2,1)} %vir_hbm.1, bf16[80,512]{1,0:T(8,128)(2,1)} %bitcast.8, f32[1,80]{1,0:T(1,128)} %bitcast.11, f32[4864]{0:T(1024)} %vir_energy_ref.3), custom_call_target="tpu_custom_call" | custom-call | flops 3187671040 | bytes 12451840 | tf_op jit(solution)/shard_map/pallas_call | solution.py:379
  65.3 9.1 %shard_map.78 = (bf16[640,4864]{1,0:T(8,128)(2,1)}, f32[8,8]{1,0:T(8,128)}) custom-call(bf16[640,4864]{1,0:T(8,128)(2,1)} %bitcast.7, bf16[512,4864]{1,0:T(8,128)(2,1)} %bitcast.14, bf16[80,512]{1,0:T(8,128)(2,1)} %bitcast.9, f32[1,80]{1,0:T(1,128)} %bitcast.12, f32[4864]{0:T(1024)} %vir_energy_ref.3, f32[1,512]{1,0:T(1,128)} %bitcast.10, ...), custom_call_target="tpu_custom_call" | custom-call | flops 3187671040 | bytes 18677760 | tf_op jit(solution)/shard_map/pallas_call | solution.py:411
